TPU v7x, 32 devices: a whole 2x2x4 slice. The times are simulated.
32 devices in a mesh: op: 8 (over y, x, core), tm: 4 (over z).
Axes of the slice: x: 2, y: 2, z: 4, core: 2. Of those that a mesh axis runs over, the one named last changes fastest.
Arguments:
- phi: bfloat16 [256, 32, 2, 128, 128], P('op', 'tm'), may hold values from -6 to 6
- tau_fwd: bfloat16 [2, 32, 2, 128, 128], P(None, 'tm'), may hold values from -0.375 to 0.375
- tau_bwd: bfloat16 [2, 32, 2, 128, 128], P(None, 'tm'), may hold values from -0.375 to 0.375
- src_times: int32 [2], replicated, may hold values from 0 to 31
- partner: int32 [256], replicated, may hold values from 0 to 255, each once
Outputs:
- corr: float32 [256, 2, 32, 2, 256], P('op', None, 'tm')
Inputs may be any that keep to these rules, and one draw needn't show every extreme that they name: partner is a permutation of the operators. `src_times`: source times may repeat.
All inputs are finite; a program needn't handle non-finite values.
Results may differ from a plain program's by a relative error of at most 0.0041.
Values may be sent and summed in bfloat16 or wider, within the bound.
No kernel may reach another device: no remote copies, remote signals or barrier semaphores. Data moves between devices by JAX's collectives and lax.ppermute only.
A program may use at most 256 MiB of HBM per device.

v0:
```python
import jax
import jax.numpy as jnp
from jax import lax
from jax.sharding import PartitionSpec as P


def from_root(value, axis, source):
    kept = jnp.where(lax.axis_index(axis) == source, value, 0).astype(value.dtype)
    return lax.psum(kept, axis)


def complex_product(spec, left_re, left_im, right_re, right_im):

    def inner(first, second):
        return jnp.einsum(spec, first, second, preferred_element_type=jnp.float32)

    return (
        inner(left_re, right_re) - inner(left_im, right_im),
        inner(left_re, right_im) + inner(left_im, right_re),
    )


def corr_block(panel, source):
    width = panel.shape[-1]
    sink_re = panel[:, :, :, 0]
    sink_im = panel[:, :, :, 1]
    source_re = source[:, :, 0]
    source_im = source[:, :, 1]

    def inner(first, second):
        return jnp.einsum("jstad,ksad->jstk", first, second, preferred_element_type=jnp.float32)

    real_part = inner(sink_re, source_re) + inner(sink_im, source_im)
    imag_part = inner(sink_im, source_re) - inner(sink_re, source_im)
    return jnp.stack([real_part, imag_part], 3) / width


def body(phi, tau_fwd, tau_bwd, src_times, partner):
    time_local = phi.shape[1]
    sources = tau_fwd.shape[0]
    left_re, left_im = complex_product(
        "stab,jtbc->jstac", tau_fwd[:, :, 0], tau_fwd[:, :, 1], phi[:, :, 0], phi[:, :, 1]
    )
    left_re = left_re.astype(jnp.bfloat16)
    left_im = left_im.astype(jnp.bfloat16)
    sink_re, sink_im = complex_product(
        "jstac,stcd->jstad", left_re, left_im, tau_bwd[:, :, 0], tau_bwd[:, :, 1]
    )
    panel = jnp.stack([sink_re.astype(jnp.bfloat16), sink_im.astype(jnp.bfloat16)], 3)
    fields = []
    for source_index in range(sources):
        when = src_times[source_index]
        local = lax.dynamic_index_in_dim(phi, when % time_local, 1, False)
        fields.append(from_root(local, "tm", when // time_local))
    own_sources = jnp.stack(fields, 1)
    mixed = corr_block(panel, lax.all_gather(own_sources, "op", axis=0, tiled=True))
    return jnp.take(mixed, partner, axis=4)


def solution(mesh):
    in_specs = (
        P("op", "tm", None, None, None),
        P(None, "tm", None, None, None),
        P(None, "tm", None, None, None),
        P(),
        P(),
    )
    out_specs = P("op", None, "tm", None, None)
    return jax.shard_map(body, mesh=mesh, in_specs=in_specs, out_specs=out_specs, check_vma=False)
```

profile of v0, /device:TPU:0, one launch (start us, length us, event | category | flops | bytes accessed | tf_op | source)
XLA Modules:
  0.0 562.1 jit_solution(6328620957796238682)
XLA Ops:
  6.5 0.0 all-reduce.3.cloned.1.call-start
  6.5 1.3 fusion.62
  13.0 2.7 constant_dynamic-slice_fusion.1
  15.8 4.6 copy_select_fusion
  20.4 0.0 all-reduce.3.cloned.1.call-update
  20.4 0.0 all-gather.2.cloned.1.call-start
  20.5 157.8 %all-reduce.3.cloned.1.call-done = (bf16[32,1,2,128,128]{4,0,3,1,2:T(8,128)(2,1)}, bf16[32,1,2,128,128]{4,0,3,1,2:T(8,128)(2,1)}) async-done(((bf16[32,1,2,128,128]{4,0,3,1,2:T(8,128)(2,1)}, bf16[32,1,2,128,128]{4,0,3,1,2:T(8,128)(2,1)}), (bf16[32,1,2,128,128]{4,0,3,1,2:T(8,128)(2,1)}, bf16[32,1,2,128,128]{4,0,3,1,2:T(8,128)(2,1)})) %all-reduce.3.cloned.1.call-update) | async-done | bytes 4194320 | tf_op jit(solution)/shard_map/psum | solution.py:9
  178.3 4.6 pad_maximum_fusion
  182.9 0.0 all-gather.2.cloned.1.call-update
  182.9 13.8 %fusion.60 = (bf16[32,8,1,128,128]{4,3,2,1,0:T(8,128)(2,1)}, bf16[32,8,1,128,128]{4,3,2,1,0:T(8,128)(2,1)}) fusion(bf16[32,8,2,128,128]{4,3,2,1,0:T(8,128)(2,1)} %param.5), kind=kLoop, calls=%fused_computation.59 | loop fusion | bytes 33554432 | tf_op jit(solution)/shard_map/slice | solution.py:42
  196.7 0.0 copy-start.2
  196.7 0.0 copy-start.1
  196.7 12.1 %copy.63 = bf16[32,8,1,128,128]{3,4,0,1,2:T(8,128)(2,1)} copy(bf16[32,8,1,128,128]{4,3,2,1,0:T(8,128)(2,1)} %get-tuple-element.10) | data formatting | bytes 16777216
  208.9 11.9 %copy.65 = bf16[32,8,1,128,128]{3,4,0,1,2:T(8,128)(2,1)} copy(bf16[32,8,1,128,128]{4,3,2,1,0:T(8,128)(2,1)} %get-tuple-element.9) | data formatting | bytes 16777216
  220.8 0.0 copy-done.2
  220.8 0.6 pad_clamp_fusion
  221.4 0.5 compare_and_fusion
  222.0 0.0 copy-done.1
  222.0 0.1 fusion.61
  222.1 19.0 %fusion.23 = f32[8,32,128,2,128]{4,2,3,1,0:T(8,128)} fusion(bf16[32,8,1,128,128]{3,4,0,1,2:T(8,128)(2,1)} %copy.63, bf16[2,8,1,128,128]{4,3,2,1,0:T(8,128)(2,1)S(1)} %get-tuple-element.12), kind=kOutput, calls=%fused_computation.26 | convolution fusion | flops 2147483648 | bytes 42467328 | tf_op jit(solution)/shard_map/stab,jtbc->jstac/dot_general | solution.py:15
  241.0 21.0 %fusion.25 = f32[8,32,128,2,128]{4,2,3,1,0:T(8,128)} fusion(bf16[32,8,1,128,128]{3,4,0,1,2:T(8,128)(2,1)} %copy.65, bf16[2,8,1,128,128]{4,3,2,1,0:T(8,128)(2,1)S(1)} %get-tuple-element.12), kind=kOutput, calls=%fused_computation.28 | convolution fusion | flops 2147483648 | bytes 42467328 | tf_op jit(solution)/shard_map/stab,jtbc->jstac/dot_general | solution.py:15
  262.0 20.4 %fusion = bf16[32,2,8,128,128]{3,4,1,0,2:T(8,128)(2,1)} fusion(f32[8,32,128,2,128]{4,2,3,1,0:T(8,128)} %fusion.23, bf16[32,8,1,128,128]{3,4,0,1,2:T(8,128)(2,1)} %copy.65, bf16[2,8,1,128,128]{4,3,2,1,0:T(8,128)(2,1)S(1)} %get-tuple-element.11), kind=kOutput, calls=%fused_computation.5 | convolution fusion | flops 2164260864 | bytes 59244544 | tf_op jit(solution)/shard_map/stab,jtbc->jstac/dot_general | solution.py:15
  282.4 0.0 copy-start
  282.4 21.5 %fusion.1 = bf16[32,2,8,128,128]{3,4,1,0,2:T(8,128)(2,1)} fusion(f32[8,32,128,2,128]{4,2,3,1,0:T(8,128)} %fusion.25, bf16[32,8,1,128,128]{3,4,0,1,2:T(8,128)(2,1)} %copy.63, bf16[2,8,1,128,128]{4,3,2,1,0:T(8,128)(2,1)S(1)} %get-tuple-element.11), kind=kOutput, calls=%fused_computation.6 | convolution fusion | flops 2164260864 | bytes 59244544 | tf_op jit(solution)/shard_map/stab,jtbc->jstac/dot_general | solution.py:15
  303.9 0.0 copy-done
  303.9 17.1 %fusion.10 = f32[2,8,32,128,128]{4,3,2,1,0:T(8,128)} fusion(bf16[32,2,8,128,128]{3,4,1,0,2:T(8,128)(2,1)} %fusion, bf16[2,8,2,128,128]{4,3,2,1,0:T(8,128)(2,1)S(1)} %copy-done), kind=kOutput, calls=%fused_computation.17 | convolution fusion | flops 2147483648 | bytes 50855936 | tf_op jit(solution)/shard_map/jstac,stcd->jstad/dot_general | solution.py:15
  320.9 17.1 %fusion.8 = f32[2,8,32,128,128]{4,3,2,1,0:T(8,128)} fusion(bf16[32,2,8,128,128]{3,4,1,0,2:T(8,128)(2,1)} %fusion, bf16[2,8,2,128,128]{4,3,2,1,0:T(8,128)(2,1)S(1)} %copy-done), kind=kOutput, calls=%fused_computation.15 | convolution fusion | flops 2147483648 | bytes 50855936 | tf_op jit(solution)/shard_map/jstac,stcd->jstad/dot_general | solution.py:15
  338.0 25.6 %fusion.16 = bf16[32,2,8,128,128]{4,3,0,2,1:T(8,128)(2,1)} fusion(f32[2,8,32,128,128]{4,3,2,1,0:T(8,128)} %fusion.10, bf16[32,2,8,128,128]{3,4,1,0,2:T(8,128)(2,1)} %fusion.1, bf16[2,8,2,128,128]{4,3,2,1,0:T(8,128)(2,1)S(1)} %copy-done), kind=kOutput, calls=%fused_computation.23 | convolution fusion | flops 2164260864 | bytes 67633152 | tf_op jit(solution)/shard_map/jstac,stcd->jstad/dot_general | solution.py:15
  363.6 23.6 %fusion.19 = bf16[32,2,8,128,128]{4,3,0,2,1:T(8,128)(2,1)} fusion(f32[2,8,32,128,128]{4,3,2,1,0:T(8,128)} %fusion.8, bf16[32,2,8,128,128]{3,4,1,0,2:T(8,128)(2,1)} %fusion.1, bf16[2,8,2,128,128]{4,3,2,1,0:T(8,128)(2,1)S(1)} %copy-done), kind=kOutput, calls=%fused_computation.24 | convolution fusion | flops 2164260864 | bytes 67633152 | tf_op jit(solution)/shard_map/jstac,stcd->jstad/dot_general | solution.py:15
  387.2 0.0 all-gather.2.cloned.1.call-done
  387.2 39.7 %fusion.31 = f32[2,256,32,8]{1,2,3,0:T(8,128)S(1)} fusion(bf16[32,2,8,128,128]{4,3,0,2,1:T(8,128)(2,1)} %fusion.16, bf16[256,2,2,128,128]{4,0,3,1,2:T(8,128)(2,1)} %all-gather.2.cloned.1.call-done), kind=kOutput, calls=%fused_computation.36 | convolution fusion | flops 4294967296 | bytes 34078720 | tf_op jit(solution)/shard_map/jstad,ksad->jstk/dot_general | solution.py:31
  426.9 39.5 %fusion.28 = f32[2,256,32,8]{1,2,3,0:T(8,128)S(1)} fusion(bf16[32,2,8,128,128]{4,3,0,2,1:T(8,128)(2,1)} %fusion.19, bf16[256,2,2,128,128]{4,0,3,1,2:T(8,128)(2,1)} %all-gather.2.cloned.1.call-done), kind=kOutput, calls=%fused_computation.35 | convolution fusion | flops 4294967296 | bytes 34078720 | tf_op jit(solution)/shard_map/jstad,ksad->jstk/dot_general | solution.py:31
  466.4 39.5 %fusion.43 = f32[32,2,8,1,256]{4,0,2,1,3:T(8,128)S(1)} fusion(f32[2,256,32,8]{1,2,3,0:T(8,128)S(1)} %fusion.31, bf16[32,2,8,128,128]{4,3,0,2,1:T(8,128)(2,1)} %fusion.19, bf16[256,2,2,128,128]{4,0,3,1,2:T(8,128)(2,1)} %all-gather.2.cloned.1.call-done), kind=kOutput, calls=%fused_computation.40 | convolution fusion | flops 4295098368 | bytes 34603008 | tf_op jit(solution)/shard_map/jstad,ksad->jstk/dot_general | solution.py:31
  506.0 0.0 copy-start.3
  506.0 32.0 %fusion.49 = f32[32,2,8,1,256]{4,0,2,1,3:T(8,128)S(1)} fusion(f32[2,256,32,8]{1,2,3,0:T(8,128)S(1)} %fusion.28, bf16[32,2,8,128,128]{4,3,0,2,1:T(8,128)(2,1)} %fusion.16, bf16[256,2,2,128,128]{4,0,3,1,2:T(8,128)(2,1)} %all-gather.2.cloned.1.call-done), kind=kOutput, calls=%fused_computation.42 | convolution fusion | flops 4295098368 | bytes 34603008 | tf_op jit(solution)/shard_map/jstad,ksad->jstk/dot_general | solution.py:31
  538.0 0.1 maximum_multiply_fusion
  538.1 2.7 copy.39
  540.8 5.4 gather_fusion
  546.2 0.0 copy-done.3
  546.2 4.0 select_bitcast_fusion
  550.2 4.8 copy.40
  (1 shorter events, 0.0 us)
Async XLA Ops:
  6.5 171.8 %all-reduce.3.cloned.1.call-start = ((), (), s32[]{:S(2)}) async-start(), calls=%async_computation.1 | async-start | bytes 8388608 | tf_op jit(solution)/shard_map/psum | solution.py:9
  20.4 366.8 %all-gather.2.cloned.1.call-start = ((), (), s32[]{:S(2)}) async-start(), calls=%async_computation | async-start | bytes 37748736 | tf_op jit(solution)/shard_map/all_gather | solution.py:56
  196.7 24.1 %copy-start.2 = (s32[256]{0:T(256)S(1)}, s32[256]{0:T(256)}, u32[]{:S(2)}) copy-start(s32[256]{0:T(256)} %param.9) | copy-start | bytes 3076
  196.7 25.2 %copy-start.1 = (bf16[2,8,2,128,128]{4,3,2,1,0:T(8,128)(2,1)S(1)}, bf16[2,8,2,128,128]{4,3,2,1,0:T(8,128)(2,1)}, u32[]{:S(2)}) copy-start(bf16[2,8,2,128,128]{4,3,2,1,0:T(8,128)(2,1)} %param.6) | copy-start | bytes 3145732
  282.4 21.5 %copy-start = (bf16[2,8,2,128,128]{4,3,2,1,0:T(8,128)(2,1)S(1)}, bf16[2,8,2,128,128]{4,3,2,1,0:T(8,128)(2,1)}, u32[]{:S(2)}) copy-start(bf16[2,8,2,128,128]{4,3,2,1,0:T(8,128)(2,1)} %param.7) | copy-start | bytes 3145732
  506.0 40.2 %copy-start.3 = (pred[256]{0:T(512)(128)(4,1)S(1)}, pred[256]{0:T(512)(128)(4,1)}, u32[]{:S(2)}) copy-start(pred[256]{0:T(512)(128)(4,1)} %compare_and_fusion) | copy-start | bytes 772
Sparse Core Ops, SparseCore 0:
  20.6 157.7 all-reduce.2
  183.0 166.2 all-gather.1
where the time goes:
time: 567 us; the launch traced here: 562 us
  matrix products  316 us (56%)
  waiting for transfers between devices  158 us (28%)
  local copies, waits for them, and re-layouts  55 us (10%)
  between operations  18.9 us (3%)
  other arithmetic  14.4 us (3%)
    dot_general x8, matrix products, inner(): return jnp.einsum(spec, first, second, preferred_element_type=jnp.float32)  165 us
    psum x1, waiting for transfers between devices, from_root(): return lax.psum(kept, axis)  158 us
    dot_general x4, matrix products, inner(): jnp.einsum('jstad,ksad->jstk', first, second, preferred_element_type=jnp....  151 us
    unnamed x10, local copies, waits for them, and re-layouts  24.1 us
    slice x1, local copies, waits for them, and re-layouts, body(): phi[:, :, 1]  13.8 us
  transfers between devices with their start and end apart: 2, of which 1 were waited for; matrix products, arithmetic and copies ran while one was open for 36% of the time, Pallas kernels for 0%

commit v1 on v0

--- a/solution.py
+++ b/solution.py
@@ -6,7 +6,7 @@
 
 def from_root(value, axis, source):
     kept = jnp.where(lax.axis_index(axis) == source, value, 0).astype(value.dtype)
-    return lax.psum(kept, axis)
+    return jnp.sum(lax.all_gather(kept, axis), axis=0)
 
 
 def complex_product(spec, left_re, left_im, right_re, right_im):

time: 567 us -> 713 us (1.26)
  waiting for transfers between devices: 158 us -> 295 us
  other arithmetic: 14.4 us -> 22.5 us
    all_gather x0 -> x2, waiting for transfers between devices: none -> 294 us  [from_root(): return jnp.sum(lax.all_gather(kept, axis), axis=0)]
    psum x1 -> x0, waiting for transfers between devices: 158 us -> none  [from_root(): return lax.psum(kept, axis)]
    reduce_sum x0 -> x2, other arithmetic: none -> 10.5 us  [from_root(): return jnp.sum(lax.all_gather(kept, axis), axis=0)]
  transfers between devices with their start and end apart: 2 -> 3, of which waited for: 1 -> 2; matrix products, arithmetic and copies ran while one was open for 36% -> 30% of each run, Pallas kernels for 0% -> 0%
where the time goes in v1:
time: 713 us; the launch traced here: 706 us
  matrix products  315 us (44%)
  waiting for transfers between devices  295 us (41%)
  local copies, waits for them, and re-layouts  54.9 us (8%)
  other arithmetic  22.5 us (3%)
  between operations  18.5 us (3%)
    all_gather x2, waiting for transfers between devices, from_root(): return jnp.sum(lax.all_gather(kept, axis), axis=0)  294 us
    dot_general x8, matrix products, inner(): return jnp.einsum(spec, first, second, preferred_element_type=jnp.float32)  164 us
    dot_general x4, matrix products, inner(): jnp.einsum('jstad,ksad->jstk', first, second, preferred_element_type=jnp....  151 us
    unnamed x10, local copies, waits for them, and re-layouts  24 us
  transfers between devices with their start and end apart: 3, of which 2 were waited for; matrix products, arithmetic and copies ran while one was open for 30% of the time, Pallas kernels for 0%

profile of v1, /device:TPU:0, one launch (start us, length us, event | category | flops | bytes accessed | tf_op | source)
XLA Modules:
  0.0 706.4 jit_solution(4931383264046168132)
XLA Ops:
  6.5 0.0 all-gather.10.cloned.1.call-start
  6.5 1.4 fusion.62
  13.0 4.5 dynamic-slice_select_fusion.1
  17.5 0.0 all-gather.10.cloned.1.call-update
  17.5 0.0 all-gather.8.cloned.1.call-start
  17.6 0.7 all-gather.8.cloned.1.call-update
  18.3 0.0 all-gather.6.cloned.1.call-start
  18.3 151.7 %all-gather.10.cloned.1.call-done = bf16[128,1,2,128,128]{4,3,2,1,0:T(8,128)(2,1)} async-done(((bf16[32,1,2,128,128]{4,3,2,1,0:T(8,128)(2,1)}), bf16[128,1,2,128,128]{4,3,2,1,0:T(8,128)(2,1)}) %all-gather.10.cloned.1.call-update) | async-done | bytes 8388624 | tf_op jit(solution)/shard_map/all_gather | solution.py:9
  170.0 5.2 bitcast_reduce_fusion
  175.3 1.4 copy.125
  176.6 142.8 %all-gather.8.cloned.1.call-done = bf16[128,1,2,128,128]{4,3,2,1,0:T(8,128)(2,1)} async-done(((bf16[32,1,2,128,128]{4,3,2,1,0:T(8,128)(2,1)}), bf16[128,1,2,128,128]{4,3,2,1,0:T(8,128)(2,1)}) %all-gather.8.cloned.1.call-update) | async-done | bytes 8388624 | tf_op jit(solution)/shard_map/all_gather | solution.py:9
  319.4 5.2 bitcast_reduce_fusion.1
  324.7 1.4 copy.126
  326.0 2.3 pad_maximum_fusion
  328.3 0.0 all-gather.6.cloned.1.call-update
  328.4 13.7 %fusion.60 = (bf16[32,8,1,128,128]{4,3,2,1,0:T(8,128)(2,1)}, bf16[32,8,1,128,128]{4,3,2,1,0:T(8,128)(2,1)}) fusion(bf16[32,8,2,128,128]{4,3,2,1,0:T(8,128)(2,1)} %param.5), kind=kLoop, calls=%fused_computation.61 | loop fusion | bytes 33554432 | tf_op jit(solution)/shard_map/slice | solution.py:42
  342.1 0.0 copy-start.2
  342.1 0.0 copy-start.1
  342.1 12.1 %copy.75 = bf16[32,8,1,128,128]{3,4,0,1,2:T(8,128)(2,1)} copy(bf16[32,8,1,128,128]{4,3,2,1,0:T(8,128)(2,1)} %get-tuple-element.8) | data formatting | bytes 16777216
  354.2 11.9 %copy.77 = bf16[32,8,1,128,128]{3,4,0,1,2:T(8,128)(2,1)} copy(bf16[32,8,1,128,128]{4,3,2,1,0:T(8,128)(2,1)} %get-tuple-element.7) | data formatting | bytes 16777216
  366.1 0.0 copy-done.2
  366.1 0.6 pad_clamp_fusion
  366.7 0.5 compare_and_fusion
  367.2 0.0 copy-done.1
  367.2 0.1 fusion.61
  367.4 19.0 %fusion.23 = f32[8,32,128,2,128]{4,2,3,1,0:T(8,128)} fusion(bf16[32,8,1,128,128]{3,4,0,1,2:T(8,128)(2,1)} %copy.75, bf16[2,8,1,128,128]{4,3,2,1,0:T(8,128)(2,1)S(1)} %get-tuple-element.10), kind=kOutput, calls=%fused_computation.26 | convolution fusion | flops 2147483648 | bytes 42467328 | tf_op jit(solution)/shard_map/stab,jtbc->jstac/dot_general | solution.py:15
  386.3 20.6 %fusion.25 = f32[8,32,128,2,128]{4,2,3,1,0:T(8,128)} fusion(bf16[32,8,1,128,128]{3,4,0,1,2:T(8,128)(2,1)} %copy.77, bf16[2,8,1,128,128]{4,3,2,1,0:T(8,128)(2,1)S(1)} %get-tuple-element.10), kind=kOutput, calls=%fused_computation.28 | convolution fusion | flops 2147483648 | bytes 42467328 | tf_op jit(solution)/shard_map/stab,jtbc->jstac/dot_general | solution.py:15
  406.9 20.3 %fusion = bf16[32,2,8,128,128]{3,4,1,0,2:T(8,128)(2,1)} fusion(f32[8,32,128,2,128]{4,2,3,1,0:T(8,128)} %fusion.23, bf16[32,8,1,128,128]{3,4,0,1,2:T(8,128)(2,1)} %copy.77, bf16[2,8,1,128,128]{4,3,2,1,0:T(8,128)(2,1)S(1)} %get-tuple-element.9), kind=kOutput, calls=%fused_computation.5 | convolution fusion | flops 2164260864 | bytes 59244544 | tf_op jit(solution)/shard_map/stab,jtbc->jstac/dot_general | solution.py:15
  427.1 0.0 copy-start
  427.1 21.3 %fusion.1 = bf16[32,2,8,128,128]{3,4,1,0,2:T(8,128)(2,1)} fusion(f32[8,32,128,2,128]{4,2,3,1,0:T(8,128)} %fusion.25, bf16[32,8,1,128,128]{3,4,0,1,2:T(8,128)(2,1)} %copy.75, bf16[2,8,1,128,128]{4,3,2,1,0:T(8,128)(2,1)S(1)} %get-tuple-element.9), kind=kOutput, calls=%fused_computation.6 | convolution fusion | flops 2164260864 | bytes 59244544 | tf_op jit(solution)/shard_map/stab,jtbc->jstac/dot_general | solution.py:15
  448.5 0.0 copy-done
  448.5 17.1 %fusion.10 = f32[2,8,32,128,128]{4,3,2,1,0:T(8,128)} fusion(bf16[32,2,8,128,128]{3,4,1,0,2:T(8,128)(2,1)} %fusion, bf16[2,8,2,128,128]{4,3,2,1,0:T(8,128)(2,1)S(1)} %copy-done), kind=kOutput, calls=%fused_computation.17 | convolution fusion | flops 2147483648 | bytes 50855936 | tf_op jit(solution)/shard_map/jstac,stcd->jstad/dot_general | solution.py:15
  465.5 17.1 %fusion.8 = f32[2,8,32,128,128]{4,3,2,1,0:T(8,128)} fusion(bf16[32,2,8,128,128]{3,4,1,0,2:T(8,128)(2,1)} %fusion, bf16[2,8,2,128,128]{4,3,2,1,0:T(8,128)(2,1)S(1)} %copy-done), kind=kOutput, calls=%fused_computation.15 | convolution fusion | flops 2147483648 | bytes 50855936 | tf_op jit(solution)/shard_map/jstac,stcd->jstad/dot_general | solution.py:15
  482.6 25.6 %fusion.16 = bf16[32,2,8,128,128]{4,3,0,2,1:T(8,128)(2,1)} fusion(f32[2,8,32,128,128]{4,3,2,1,0:T(8,128)} %fusion.10, bf16[32,2,8,128,128]{3,4,1,0,2:T(8,128)(2,1)} %fusion.1, bf16[2,8,2,128,128]{4,3,2,1,0:T(8,128)(2,1)S(1)} %copy-done), kind=kOutput, calls=%fused_computation.23 | convolution fusion | flops 2164260864 | bytes 67633152 | tf_op jit(solution)/shard_map/jstac,stcd->jstad/dot_general | solution.py:15
  508.2 23.6 %fusion.19 = bf16[32,2,8,128,128]{4,3,0,2,1:T(8,128)(2,1)} fusion(f32[2,8,32,128,128]{4,3,2,1,0:T(8,128)} %fusion.8, bf16[32,2,8,128,128]{3,4,1,0,2:T(8,128)(2,1)} %fusion.1, bf16[2,8,2,128,128]{4,3,2,1,0:T(8,128)(2,1)S(1)} %copy-done), kind=kOutput, calls=%fused_computation.24 | convolution fusion | flops 2164260864 | bytes 67633152 | tf_op jit(solution)/shard_map/jstac,stcd->jstad/dot_general | solution.py:15
  531.8 0.0 all-gather.6.cloned.1.call-done
  531.8 39.5 %fusion.31 = f32[2,256,32,8]{1,2,3,0:T(8,128)S(1)} fusion(bf16[32,2,8,128,128]{4,3,0,2,1:T(8,128)(2,1)} %fusion.16, bf16[256,2,2,128,128]{4,0,3,1,2:T(8,128)(2,1)} %all-gather.6.cloned.1.call-done), kind=kOutput, calls=%fused_computation.40 | convolution fusion | flops 4294967296 | bytes 34078720 | tf_op jit(solution)/shard_map/jstad,ksad->jstk/dot_general | solution.py:31
  571.3 39.6 %fusion.28 = f32[2,256,32,8]{1,2,3,0:T(8,128)S(1)} fusion(bf16[32,2,8,128,128]{4,3,0,2,1:T(8,128)(2,1)} %fusion.19, bf16[256,2,2,128,128]{4,0,3,1,2:T(8,128)(2,1)} %all-gather.6.cloned.1.call-done), kind=kOutput, calls=%fused_computation.39 | convolution fusion | flops 4294967296 | bytes 34078720 | tf_op jit(solution)/shard_map/jstad,ksad->jstk/dot_general | solution.py:31
  610.9 39.8 %fusion.43 = f32[32,2,8,1,256]{4,0,2,1,3:T(8,128)S(1)} fusion(f32[2,256,32,8]{1,2,3,0:T(8,128)S(1)} %fusion.31, bf16[32,2,8,128,128]{4,3,0,2,1:T(8,128)(2,1)} %fusion.19, bf16[256,2,2,128,128]{4,0,3,1,2:T(8,128)(2,1)} %all-gather.6.cloned.1.call-done), kind=kOutput, calls=%fused_computation.44 | convolution fusion | flops 4295098368 | bytes 34603008 | tf_op jit(solution)/shard_map/jstad,ksad->jstk/dot_general | solution.py:31
  650.7 0.0 copy-start.3
  650.7 31.9 %fusion.49 = f32[32,2,8,1,256]{4,0,2,1,3:T(8,128)S(1)} fusion(f32[2,256,32,8]{1,2,3,0:T(8,128)S(1)} %fusion.28, bf16[32,2,8,128,128]{4,3,0,2,1:T(8,128)(2,1)} %fusion.16, bf16[256,2,2,128,128]{4,0,3,1,2:T(8,128)(2,1)} %all-gather.6.cloned.1.call-done), kind=kOutput, calls=%fused_computation.46 | convolution fusion | flops 4295098368 | bytes 34603008 | tf_op jit(solution)/shard_map/jstad,ksad->jstk/dot_general | solution.py:31
  682.7 0.1 maximum_multiply_fusion
  682.8 2.7 copy.53
  685.5 5.4 gather_fusion
  690.9 0.0 copy-done.3
  690.9 4.0 select_bitcast_fusion
  694.9 4.8 copy.54
  (1 shorter events, 0.0 us)
Async XLA Ops:
  6.5 163.5 %all-gather.10.cloned.1.call-start = ((), (), s32[]{:S(2)}) async-start(), calls=%async_computation.2 | async-start | bytes 10485760 | tf_op jit(solution)/shard_map/all_gather | solution.py:9
  17.5 301.9 %all-gather.8.cloned.1.call-start = ((), (), s32[]{:S(2)}) async-start(), calls=%async_computation.1 | async-start | bytes 10485760 | tf_op jit(solution)/shard_map/all_gather | solution.py:9
  18.3 513.5 %all-gather.6.cloned.1.call-start = ((), (), s32[]{:S(2)}) async-start(), calls=%async_computation | async-start | bytes 37748736 | tf_op jit(solution)/shard_map/all_gather | solution.py:56
  342.1 24.0 %copy-start.2 = (s32[256]{0:T(256)S(1)}, s32[256]{0:T(256)}, u32[]{:S(2)}) copy-start(s32[256]{0:T(256)} %param.9) | copy-start | bytes 3076
  342.1 25.1 %copy-start.1 = (bf16[2,8,2,128,128]{4,3,2,1,0:T(8,128)(2,1)S(1)}, bf16[2,8,2,128,128]{4,3,2,1,0:T(8,128)(2,1)}, u32[]{:S(2)}) copy-start(bf16[2,8,2,128,128]{4,3,2,1,0:T(8,128)(2,1)} %param.6) | copy-start | bytes 3145732
  427.1 21.3 %copy-start = (bf16[2,8,2,128,128]{4,3,2,1,0:T(8,128)(2,1)S(1)}, bf16[2,8,2,128,128]{4,3,2,1,0:T(8,128)(2,1)}, u32[]{:S(2)}) copy-start(bf16[2,8,2,128,128]{4,3,2,1,0:T(8,128)(2,1)} %param.7) | copy-start | bytes 3145732
  650.7 40.2 %copy-start.3 = (pred[256]{0:T(512)(128)(4,1)S(1)}, pred[256]{0:T(512)(128)(4,1)}, u32[]{:S(2)}) copy-start(pred[256]{0:T(512)(128)(4,1)} %compare_and_fusion) | copy-start | bytes 772
Sparse Core Ops, SparseCore 0:
  17.6 152.3 all-gather.9
  171.6 147.7 all-gather.7
  328.5 165.5 all-gather.5
